TPU v7x, 256 devices: a whole 4x4x8 slice. The times are simulated.
256 devices in a mesh: freq: 32 (over z, x), rcv: 8 (over y, core).
Axes of the slice: x: 4, y: 4, z: 8, core: 2. Of those that a mesh axis runs over, the one named last changes fastest.
Arguments:
- primaries_start: float32 [512, 1024, 128], P(('rcv', 'freq')), may hold values from -6 to 6
- surface_operator: bfloat16 [512, 2, 384, 512], P('freq', None, 'rcv'), may hold values from -0.25 to 0.25
- data_spectra: bfloat16 [384, 512, 2, 128], P('rcv', 'freq'), may hold values from -6 to 6
- shrinkage: float32 [128], replicated, may hold values from 0.2 to 2
Outputs:
- primaries: float32 [512, 1024, 128], P(('rcv', 'freq'))
- residual_spectra: bfloat16 [384, 512, 2, 128], P('rcv', 'freq')
All inputs are finite; a program needn't handle non-finite values.
Results may differ from a plain program's by a relative error of at most 0.0085.
Values may be sent and summed in bfloat16 or wider, within the bound.
No kernel may reach another device: no remote copies, remote signals or barrier semaphores. Data moves between devices by JAX's collectives and lax.ppermute only.
A program may use at most 64 MiB of HBM per device.

v0:
```python
import math
import jax
import jax.numpy as jnp
from jax import lax
from jax.sharding import PartitionSpec as P

S = 128
NS = 512
T_SIZE = 1024
ITERS = 2
NF = 512


def transform_table(frequencies, samples):
    freq_index = jnp.arange(frequencies, dtype=jnp.int32)[:, None]
    sample_index = jnp.arange(samples, dtype=jnp.int32)[None, :]
    phase = freq_index * sample_index % samples
    angle = phase.astype(jnp.float32) * (2.0 * math.pi / samples)
    factor = math.sqrt(2.0 / samples)
    return jnp.stack([factor * jnp.cos(angle), -factor * jnp.sin(angle)], axis=1).astype(
        jnp.bfloat16
    )


def forward_product(block, piece):
    real_op = block[:, 0]
    imag_op = block[:, 1]
    real_in = piece[:, :, 0]
    imag_in = piece[:, :, 1]

    def product(left, right):
        return jnp.einsum("krn,nks->rks", left, right, preferred_element_type=jnp.float32)

    real_out = product(real_op, real_in) - product(imag_op, imag_in)
    imag_out = product(real_op, imag_in) + product(imag_op, real_in)
    return jnp.stack([real_out, imag_out], axis=2)


def adjoint_product(block, resid):
    real_op = block[:, 0]
    imag_op = block[:, 1]
    real_res = resid[:, :, 0]
    imag_res = resid[:, :, 1]

    def product(left, right):
        return jnp.einsum("krn,rks->nks", left, right, preferred_element_type=jnp.float32)

    real_dir = product(real_op, real_res) + product(imag_op, imag_res)
    imag_dir = product(real_op, imag_res) - product(imag_op, real_res)
    return jnp.stack([real_dir, imag_dir], axis=2)


def local(primaries_start, surface_operator, data_spectra, shrinkage):
    table = transform_table(NF, T_SIZE)
    primaries = primaries_start
    count_total = 2.0 * NF * NS * S
    residual = data_spectra
    for iteration in range(ITERS):
        local_spectra = jnp.einsum(
            "kct,nts->nkcs",
            table,
            primaries.astype(jnp.bfloat16),
            preferred_element_type=jnp.float32,
        ).astype(jnp.bfloat16)
        spectra = lax.all_to_all(local_spectra, "freq", split_axis=1, concat_axis=0, tiled=True)
        predicted = forward_product(
            surface_operator, lax.all_gather(spectra, "rcv", axis=0, tiled=True)
        )
        residual = (data_spectra.astype(jnp.float32) - predicted).astype(jnp.bfloat16)
        residual_sq = jnp.sum(jnp.square(residual.astype(jnp.float32)))
        direction = lax.psum_scatter(
            adjoint_product(surface_operator, residual), "rcv", scatter_dimension=0, tiled=True
        )
        direction_sq = jnp.sum(jnp.square(direction))
        residual_norm, direction_norm = lax.psum((residual_sq, direction_sq), ("freq", "rcv"))
        step_size = 0.5 * residual_norm / (direction_norm + 1e-06)
        threshold = shrinkage[None, None, :] * (step_size * jnp.sqrt(direction_norm / count_total))
        direction_low = direction.astype(jnp.bfloat16)
        update = jnp.einsum(
            "kct,nkcs->nts",
            table,
            lax.all_to_all(direction_low, "freq", split_axis=0, concat_axis=1, tiled=True),
            preferred_element_type=jnp.float32,
        )
        moved = primaries + step_size * update
        primaries = moved - jnp.clip(moved, -threshold, threshold)
    return (primaries, residual)


def solution(mesh):
    return jax.shard_map(
        local,
        mesh=mesh,
        in_specs=(
            P(("rcv", "freq"), None, None),
            P("freq", None, "rcv", None),
            P("rcv", "freq", None, None),
            P(),
        ),
        out_specs=(P(("rcv", "freq"), None, None), P("rcv", "freq", None, None)),
        check_vma=False,
    )
```

profile of v0, /device:TPU:1, one launch (start us, length us, event | category | flops | bytes accessed | tf_op | source)
XLA Modules:
  0.0 497.7 jit_solution(7442395549814731971)
XLA Ops:
  7.2 8.6 %multiply_convert_fusion = (bf16[512,1,1024]{2,0,1:T(8,128)(2,1)S(1)}, bf16[512,1,1024]{2,0,1:T(8,128)(2,1)S(1)}) fusion(), kind=kLoop, calls=%fused_computation.25 | loop fusion | flops 9437184 | bytes 2097152 | tf_op jit(solution)/shard_map/convert.1
  15.8 1.0 copy-done.5
  16.8 0.7 fusion.52
  17.5 0.5 copy.32
  18.1 27.9 %all_to_all.72 = bf16[2,512,2,128]{3,0,2,1:T(2,128)(2,1)S(1)} all-to-all(bf16[2,512,2,128]{3,0,2,1:T(2,128)(2,1)S(1)} %copy.32), channel_id=1, replica_groups=mesh['freq'=32,'rcv'=8] {'freq'}, dimensions={1} | all-to-all | bytes 1048576 | tf_op jit(solution)/shard_map/all_to_all | solution.py:65
  46.0 1.4 copy.33
  47.5 33.2 %all-gather.3.cloned.1.call-done = bf16[512,16,2,128]{3,0,1,2:T(8,128)(2,1)} async-done(((bf16[64,16,2,128]{3,0,1,2:T(8,128)(2,1)}), bf16[512,16,2,128]{3,0,1,2:T(8,128)(2,1)}) %all-gather.3.cloned.1.call-update) | async-done | bytes 4194320 | tf_op jit(solution)/shard_map/all_gather | solution.py:67
  80.6 2.2 fusion.14
  82.8 2.0 fusion.15
  84.9 0.5 fusion.65
  85.4 0.5 fusion.63
  85.9 0.5 copy-done.3
  86.4 0.8 multiply_reduce_fusion.3
  87.2 0.7 fusion.88
  88.0 0.8 fusion.86
  88.8 0.8 add_bitcast_fusion.1
  89.5 0.8 subtract_bitcast_fusion.1
  90.3 4.2 pad_maximum_fusion
  94.5 10.3 %copy.36 = f32[512,16,2,128]{3,1,2,0:T(8,128)} copy(f32[512,16,2,128]{0,3,1,2:T(8,128)} %pad_maximum_fusion) | data formatting | bytes 16777216 | tf_op jit(solution)/shard_map/stack | solution.py:50
  104.9 54.2 %reduce-scatter.3.cloned.1.call-done = f32[64,16,2,128]{3,1,2,0:T(8,128)} async-done(((f32[512,16,2,128]{3,1,2,0:T(8,128)}), f32[64,16,2,128]{3,1,2,0:T(8,128)}) %reduce-scatter.3.cloned.1.call-update) | async-done | bytes 1048592 | tf_op jit(solution)/shard_map/reduce_scatter | solution.py:71
  159.1 3.4 multiply_reduce_fusion.1
  162.4 9.5 %all-to-all-start.1 = ((bf16[64,16,2,128]{3,1,2,0:T(8,128)(2,1)}), bf16[64,16,2,128]{3,1,2,0:T(8,128)(2,1)S(1)}, u32[]{:S(2)}, u32[]{:S(2)}) async-start(bf16[64,16,2,128]{3,1,2,0:T(8,128)(2,1)} %get-tuple-element.23), calls=%async_computation.2 | async-start | bytes 1048576 | tf_op jit(solution)/shard_map/all_to_all | solution.py:82
  172.0 1.3 copy.39
  173.3 77.2 %all-reduce.1 = (f32[]{:T(128)}, f32[]{:T(128)}) all-reduce(f32[]{:T(128)} %get-tuple-element.18, f32[]{:T(128)} %get-tuple-element.22), channel_id=1, replica_groups=mesh['freq'=32,'rcv'=8] {'freq','rcv'}, use_global_device_ids=true, to_apply=%region_1.2 | all-reduce | flops 2 | bytes 16 | tf_op jit(solution)/shard_map/psum | solution.py:75
  252.7 2.8 minimum_subtract_fusion.1
  255.5 1.0 copy-done.11
  256.5 1.6 fusion.55
  258.0 1.3 copy.40
  259.4 22.7 %all_to_all.73 = bf16[2,512,2,128]{3,2,0,1:T(2,128)(2,1)S(1)} all-to-all(bf16[2,512,2,128]{3,2,0,1:T(2,128)(2,1)S(1)} %copy.40), channel_id=1, replica_groups=mesh['freq'=32,'rcv'=8] {'freq'}, dimensions={1} | all-to-all | bytes 1048576 | tf_op jit(solution)/shard_map/all_to_all | solution.py:65
  282.1 1.3 copy.42
  283.5 30.9 %all-gather.5.cloned.1.call-done = bf16[512,16,2,128]{3,0,1,2:T(8,128)(2,1)} async-done(((bf16[64,16,2,128]{3,0,1,2:T(8,128)(2,1)}), bf16[512,16,2,128]{3,0,1,2:T(8,128)(2,1)}) %all-gather.5.cloned.1.call-update) | async-done | bytes 4194320 | tf_op jit(solution)/shard_map/all_gather | solution.py:67
  314.5 2.2 fusion.18
  316.7 2.0 fusion.19
  318.7 0.5 fusion.61
  319.7 0.9 multiply_reduce_fusion.2
  320.7 0.8 fusion.82
  321.4 0.8 fusion.80
  322.2 0.8 add_bitcast_fusion
  322.9 0.8 subtract_bitcast_fusion
  323.7 4.2 pad_maximum_fusion.1
  327.9 10.3 %copy.43 = f32[512,16,2,128]{3,1,2,0:T(8,128)} copy(f32[512,16,2,128]{0,3,1,2:T(8,128)} %pad_maximum_fusion.1) | data formatting | bytes 16777216 | tf_op jit(solution)/shard_map/stack | solution.py:50
  338.3 54.2 %reduce-scatter.5.cloned.1.call-done = f32[64,16,2,128]{3,1,2,0:T(8,128)} async-done(((f32[512,16,2,128]{3,1,2,0:T(8,128)}), f32[64,16,2,128]{3,1,2,0:T(8,128)}) %reduce-scatter.5.cloned.1.call-update) | async-done | bytes 1048592 | tf_op jit(solution)/shard_map/reduce_scatter | solution.py:71
  392.5 3.4 multiply_reduce_fusion
  395.8 9.5 %all-to-all-start.3 = ((bf16[64,16,2,128]{3,1,2,0:T(8,128)(2,1)}), bf16[64,16,2,128]{3,1,2,0:T(8,128)(2,1)S(1)}, u32[]{:S(2)}, u32[]{:S(2)}) async-start(bf16[64,16,2,128]{3,1,2,0:T(8,128)(2,1)} %get-tuple-element.21), calls=%async_computation.5 | async-start | bytes 1048576 | tf_op jit(solution)/shard_map/all_to_all | solution.py:82
  405.4 1.2 copy.47
  406.5 77.0 %all-reduce = (f32[]{:T(128)}, f32[]{:T(128)}) all-reduce(f32[]{:T(128)} %get-tuple-element.14, f32[]{:T(128)} %get-tuple-element.20), channel_id=1, replica_groups=mesh['freq'=32,'rcv'=8] {'freq','rcv'}, use_global_device_ids=true, to_apply=%region_6.7 | all-reduce | flops 2 | bytes 16 | tf_op jit(solution)/shard_map/psum | solution.py:75
  485.7 3.0 minimum_subtract_fusion
  488.6 2.5 copy.46
  (37 shorter events, 0.9 us)
Async XLA Ops:
  7.2 9.6 %copy-start.4 = (f32[2,1024,128]{2,1,0:T(8,128)S(1)}, f32[2,1024,128]{2,1,0:T(8,128)}, u32[]{:S(2)}) copy-start(f32[2,1024,128]{2,1,0:T(8,128)} %param.4) | copy-start | bytes 3145732
  7.2 73.5 %all-gather.3.cloned.1.call-start = ((), (), s32[]{:S(2)}) async-start(), calls=%async_computation.6 | async-start | bytes 4718592 | tf_op jit(solution)/shard_map/all_gather | solution.py:67
  15.8 1.0 copy-start.5
  15.8 1.7 copy-start.7
  17.5 63.1 %copy-start = (bf16[16,2,48,512]{3,2,1,0:T(8,128)(2,1)S(1)}, bf16[16,2,48,512]{3,2,1,0:T(8,128)(2,1)}, u32[]{:S(2)}) copy-start(bf16[16,2,48,512]{3,2,1,0:T(8,128)(2,1)} %param.5) | copy-start | bytes 4718596
  47.4 111.6 %reduce-scatter.3.cloned.1.call-start = ((), (), s32[]{:S(2)}) async-start(), calls=%async_computation.7 | async-start | bytes 9437184 | tf_op jit(solution)/shard_map/reduce_scatter | solution.py:71
  80.6 4.3 copy-start.1
  85.4 1.0 copy-start.3
  104.8 147.8 %copy-start.10 = (f32[128]{0:T(128)S(1)}, f32[128]{0:T(128)}, u32[]{:S(2)}) copy-start(f32[128]{0:T(128)} %param.7) | copy-start | bytes 1540
  162.4 90.2 %all-to-all-start.1 = ((bf16[64,16,2,128]{3,1,2,0:T(8,128)(2,1)}), bf16[64,16,2,128]{3,1,2,0:T(8,128)(2,1)S(1)}, u32[]{:S(2)}, u32[]{:S(2)}) async-start(bf16[64,16,2,128]{3,1,2,0:T(8,128)(2,1)} %get-tuple-element.23), calls=%async_computation.2 | async-start | bytes 1048576 | tf_op jit(solution)/shard_map/all_to_all | solution.py:82
  172.0 142.5 %all-gather.5.cloned.1.call-start = ((), (), s32[]{:S(2)}) async-start(), calls=%async_computation.8 | async-start | bytes 4718592 | tf_op jit(solution)/shard_map/all_gather | solution.py:67
  252.7 3.8 copy-start.6
  252.7 3.8 copy-start.8
  255.5 1.0 copy-start.11
  283.5 109.0 %reduce-scatter.5.cloned.1.call-start = ((), (), s32[]{:S(2)}) async-start(), calls=%async_computation.9 | async-start | bytes 9437184 | tf_op jit(solution)/shard_map/reduce_scatter | solution.py:71
  314.5 4.3 copy-start.2
  338.2 147.4 %copy-start.9 = (bf16[512,1,1024]{2,0,1:T(8,128)(2,1)S(1)}, bf16[512,1,1024]{2,0,1:T(8,128)(2,1)}, u32[]{:S(2)}) copy-start(bf16[512,1,1024]{2,0,1:T(8,128)(2,1)} %copy-done.7) | copy-start | bytes 3145732
  395.8 89.8 %all-to-all-start.3 = ((bf16[64,16,2,128]{3,1,2,0:T(8,128)(2,1)}), bf16[64,16,2,128]{3,1,2,0:T(8,128)(2,1)S(1)}, u32[]{:S(2)}, u32[]{:S(2)}) async-start(bf16[64,16,2,128]{3,1,2,0:T(8,128)(2,1)} %get-tuple-element.21), calls=%async_computation.5 | async-start | bytes 1048576 | tf_op jit(solution)/shard_map/all_to_all | solution.py:82
Sparse Core Ops, SparseCore 0:
  47.5 33.0 all-gather.2
  105.0 54.0 reduce-scatter.2
  283.6 30.8 all-gather.4
  338.4 54.0 reduce-scatter.4
where the time goes:
time: 499 us; the launch traced here: 498 us
  blocking collectives  205 us (41%)
  waiting for transfers between devices  173 us (35%)
  local copies, waits for them, and re-layouts  32.7 us (7%)
  other arithmetic  25.5 us (5%)
  matrix products  24.5 us (5%)
  starting transfers between devices  19.2 us (4%)
  between operations  18.3 us (4%)
    psum x2, blocking collectives, local(): lax.psum((residual_sq, direction_sq), ('freq', 'rcv'))  154 us
    reduce_scatter x2, waiting for transfers between devices, local(): lax.psum_scatter(adjoint_product(surface_operator, residual), 'rcv', scat...  108 us
    all_gather x2, waiting for transfers between devices, local(): lax.all_gather(spectra, 'rcv', axis=0, tiled=True)  64.1 us
    all_to_all x2, blocking collectives, local(): lax.all_to_all(local_spectra, 'freq', split_axis=1, concat_axis=0, tiled=...  50.6 us
    another operation x2, local copies, waits for them, and re-layouts, adjoint_product(): return jnp.stack([real_dir, imag_dir], axis=2)  20.6 us
    all_to_all x2, starting transfers between devices, local(): lax.all_to_all(direction_low, 'freq', split_axis=0, concat_axis=1, tiled=...  19.1 us
    dot_general x8, matrix products, product(): jnp.einsum('krn,nks->rks', left, right, preferred_element_type=jnp.float32)  10.5 us
  transfers between devices with their start and end apart: 6, of which 4 were waited for; matrix products, arithmetic and copies ran while one was open for 0% of the time, Pallas kernels for 0%

commit v1 on v0

--- a/solution.py
+++ b/solution.py
@@ -63,9 +63,13 @@
             preferred_element_type=jnp.float32,
         ).astype(jnp.bfloat16)
         spectra = lax.all_to_all(local_spectra, "freq", split_axis=1, concat_axis=0, tiled=True)
-        predicted = forward_product(
-            surface_operator, lax.all_gather(spectra, "rcv", axis=0, tiled=True)
+        pair_leaf_on = lambda body: jnp.concatenate(
+            lax.all_to_all(
+                jnp.stack([body for _ in range(lax.axis_size("rcv"))], axis=0), "rcv", 0, 0
+            ),
+            0,
         )
+        predicted = forward_product(surface_operator, pair_leaf_on(spectra))
         residual = (data_spectra.astype(jnp.float32) - predicted).astype(jnp.bfloat16)
         residual_sq = jnp.sum(jnp.square(residual.astype(jnp.float32)))
         direction = lax.psum_scatter(

time: 499 us -> 529 us (1.060)
  blocking collectives: 205 us -> 313 us
  waiting for transfers between devices: 173 us -> 98.5 us
  matrix products: 24.5 us -> 17.8 us
    all_to_all x0 -> x2, blocking collectives: none -> 109 us  [local(): lax.all_to_all(jnp.stack([body for _ in range(lax.axis_size('rcv'))], axi...]
    all_gather x2 -> x0, waiting for transfers between devices: 64.1 us -> none  [local(): lax.all_gather(spectra, 'rcv', axis=0, tiled=True)]
    reduce_scatter x2, waiting for transfers between devices: 108 us -> 98.5 us  [local(): lax.psum_scatter(adjoint_product(surface_operator, residual), 'rcv', scat...]
    dot_general x8, matrix products: 10.5 us -> 3.76 us  [product(): jnp.einsum('krn,nks->rks', left, right, preferred_element_type=jnp.float32)]
  transfers between devices with their start and end apart: 6 -> 4, of which waited for: 4 -> 2; matrix products, arithmetic and copies ran while one was open for 0% -> 0% of each run, Pallas kernels for 0% -> 0%
where the time goes in v1:
time: 529 us; the launch traced here: 528 us
  blocking collectives  313 us (59%)
  waiting for transfers between devices  98.5 us (19%)
  local copies, waits for them, and re-layouts  35.5 us (7%)
  other arithmetic  25.2 us (5%)
  starting transfers between devices  19.3 us (4%)
  between operations  18.2 us (3%)
  matrix products  17.8 us (3%)
    psum x2, blocking collectives, local(): lax.psum((residual_sq, direction_sq), ('freq', 'rcv'))  154 us
    all_to_all x2, blocking collectives, local(): lax.all_to_all(jnp.stack([body for _ in range(lax.axis_size('rcv'))], axi...  109 us
    reduce_scatter x2, waiting for transfers between devices, local(): lax.psum_scatter(adjoint_product(surface_operator, residual), 'rcv', scat...  98.5 us
    all_to_all x2, blocking collectives, local(): lax.all_to_all(local_spectra, 'freq', split_axis=1, concat_axis=0, tiled=...  50.3 us
    another operation x2, local copies, waits for them, and re-layouts, adjoint_product(): return jnp.stack([real_dir, imag_dir], axis=2)  20.6 us
    all_to_all x2, starting transfers between devices, local(): lax.all_to_all(direction_low, 'freq', split_axis=0, concat_axis=1, tiled=...  19.1 us
  transfers between devices with their start and end apart: 4, of which 2 were waited for; matrix products, arithmetic and copies ran while one was open for 0% of the time, Pallas kernels for 0%

profile of v1, /device:TPU:1, one launch (start us, length us, event | category | flops | bytes accessed | tf_op | source)
XLA Modules:
  0.0 528.1 jit_solution(3332944008992286740)
XLA Ops:
  7.2 8.6 %multiply_convert_fusion = (bf16[512,1,1024]{2,0,1:T(8,128)(2,1)S(1)}, bf16[512,1,1024]{2,0,1:T(8,128)(2,1)S(1)}) fusion(), kind=kLoop, calls=%fused_computation.25 | loop fusion | flops 9437184 | bytes 2097152 | tf_op jit(solution)/shard_map/convert.1
  15.8 1.0 copy-done.3
  16.8 0.7 fusion.52
  17.6 0.5 copy.52
  18.1 27.9 %all_to_all.76 = bf16[2,512,2,128]{3,0,2,1:T(2,128)(2,1)S(1)} all-to-all(bf16[2,512,2,128]{3,0,2,1:T(2,128)(2,1)S(1)} %copy.52), channel_id=1, replica_groups=mesh['freq'=32,'rcv'=8] {'freq'}, dimensions={1} | all-to-all | bytes 1048576 | tf_op jit(solution)/shard_map/all_to_all | solution.py:65
  46.4 1.1 stack.70
  47.5 55.3 %all_to_all.77 = bf16[8,64,16,2,128]{4,1,2,3,0:T(8,128)(2,1)S(1)} all-to-all(bf16[8,64,16,2,128]{4,1,2,3,0:T(8,128)(2,1)S(1)} %stack.70), channel_id=1, replica_groups=mesh['freq'=32,'rcv'=8] {'rcv'}, dimensions={0} | all-to-all | bytes 8388608 | tf_op jit(solution)/shard_map/all_to_all | solution.py:67
  102.8 1.4 copy.56
  105.1 0.5 fusion.65
  105.6 0.5 fusion.63
  106.1 0.5 copy-done.1
  106.6 0.8 multiply_reduce_fusion.3
  107.5 0.8 fusion.88
  108.2 0.8 fusion.86
  109.0 0.8 add_bitcast_fusion.1
  109.7 0.8 subtract_bitcast_fusion.1
  110.5 4.2 pad_maximum_fusion
  114.7 10.3 %copy.59 = f32[512,16,2,128]{3,1,2,0:T(8,128)} copy(f32[512,16,2,128]{0,3,1,2:T(8,128)} %pad_maximum_fusion) | data formatting | bytes 16777216 | tf_op jit(solution)/shard_map/stack | solution.py:50
  125.0 49.2 %reduce-scatter.3.cloned.1.call-done = f32[64,16,2,128]{3,1,2,0:T(8,128)} async-done(((f32[512,16,2,128]{3,1,2,0:T(8,128)}), f32[64,16,2,128]{3,1,2,0:T(8,128)}) %reduce-scatter.3.cloned.1.call-update) | async-done | bytes 1048592 | tf_op jit(solution)/shard_map/reduce_scatter | solution.py:75
  174.3 3.2 multiply_reduce_fusion.1
  177.5 9.5 %all-to-all-start.2 = ((bf16[64,16,2,128]{3,1,2,0:T(8,128)(2,1)}), bf16[64,16,2,128]{3,1,2,0:T(8,128)(2,1)S(1)}, u32[]{:S(2)}, u32[]{:S(2)}) async-start(bf16[64,16,2,128]{3,1,2,0:T(8,128)(2,1)} %get-tuple-element.25), calls=%async_computation.3 | async-start | bytes 1048576 | tf_op jit(solution)/shard_map/all_to_all | solution.py:86
  187.3 1.3 copy.62
  188.6 77.1 %all-reduce.1 = (f32[]{:T(128)}, f32[]{:T(128)}) all-reduce(f32[]{:T(128)} %get-tuple-element.20, f32[]{:T(128)} %get-tuple-element.24), channel_id=1, replica_groups=mesh['freq'=32,'rcv'=8] {'freq','rcv'}, use_global_device_ids=true, to_apply=%region_1.2 | all-reduce | flops 2 | bytes 16 | tf_op jit(solution)/shard_map/psum | solution.py:79
  267.8 2.8 minimum_subtract_fusion.1
  270.6 1.0 copy-done.9
  271.6 1.5 fusion.55
  273.1 1.3 copy.63
  274.4 22.4 %all_to_all.78 = bf16[2,512,2,128]{3,2,0,1:T(2,128)(2,1)S(1)} all-to-all(bf16[2,512,2,128]{3,2,0,1:T(2,128)(2,1)S(1)} %copy.63), channel_id=1, replica_groups=mesh['freq'=32,'rcv'=8] {'freq'}, dimensions={1} | all-to-all | bytes 1048576 | tf_op jit(solution)/shard_map/all_to_all | solution.py:65
  297.1 1.1 stack.78
  298.2 53.5 %all_to_all.79 = bf16[8,64,16,2,128]{4,1,2,3,0:T(8,128)(2,1)S(1)} all-to-all(bf16[8,64,16,2,128]{4,1,2,3,0:T(8,128)(2,1)S(1)} %stack.78), channel_id=1, replica_groups=mesh['freq'=32,'rcv'=8] {'rcv'}, dimensions={0} | all-to-all | bytes 8388608 | tf_op jit(solution)/shard_map/all_to_all | solution.py:67
  351.7 1.4 copy.67
  353.1 0.5 fusion.18
  354.1 0.5 fusion.61
  354.6 0.5 fusion.59
  355.0 0.9 multiply_reduce_fusion.2
  355.9 0.8 fusion.82
  356.7 0.8 fusion.80
  357.4 0.8 add_bitcast_fusion
  358.2 0.8 subtract_bitcast_fusion
  358.9 4.2 pad_maximum_fusion.1
  363.2 10.3 %copy.68 = f32[512,16,2,128]{3,1,2,0:T(8,128)} copy(f32[512,16,2,128]{0,3,1,2:T(8,128)} %pad_maximum_fusion.1) | data formatting | bytes 16777216 | tf_op jit(solution)/shard_map/stack | solution.py:50
  373.5 49.3 %reduce-scatter.5.cloned.1.call-done = f32[64,16,2,128]{3,1,2,0:T(8,128)} async-done(((f32[512,16,2,128]{3,1,2,0:T(8,128)}), f32[64,16,2,128]{3,1,2,0:T(8,128)}) %reduce-scatter.5.cloned.1.call-update) | async-done | bytes 1048592 | tf_op jit(solution)/shard_map/reduce_scatter | solution.py:75
  422.8 3.2 multiply_reduce_fusion
  426.0 9.5 %all-to-all-start.5 = ((bf16[64,16,2,128]{3,1,2,0:T(8,128)(2,1)}), bf16[64,16,2,128]{3,1,2,0:T(8,128)(2,1)S(1)}, u32[]{:S(2)}, u32[]{:S(2)}) async-start(bf16[64,16,2,128]{3,1,2,0:T(8,128)(2,1)} %get-tuple-element.23), calls=%async_computation.7 | async-start | bytes 1048576 | tf_op jit(solution)/shard_map/all_to_all | solution.py:86
  435.5 1.2 copy.72
  436.7 77.2 %all-reduce = (f32[]{:T(128)}, f32[]{:T(128)}) all-reduce(f32[]{:T(128)} %get-tuple-element.16, f32[]{:T(128)} %get-tuple-element.22), channel_id=1, replica_groups=mesh['freq'=32,'rcv'=8] {'freq','rcv'}, use_global_device_ids=true, to_apply=%region_6.7 | all-reduce | flops 2 | bytes 16 | tf_op jit(solution)/shard_map/psum | solution.py:79
  515.7 3.0 minimum_subtract_fusion
  518.7 2.5 copy.71
  (36 shorter events, 2.5 us)
Async XLA Ops:
  7.2 9.7 %copy-start.2 = (f32[2,1024,128]{2,1,0:T(8,128)S(1)}, f32[2,1024,128]{2,1,0:T(8,128)}, u32[]{:S(2)}) copy-start(f32[2,1024,128]{2,1,0:T(8,128)} %param.4) | copy-start | bytes 3145732
  7.2 167.1 %reduce-scatter.3.cloned.1.call-start = ((), (), s32[]{:S(2)}) async-start(), calls=%async_computation.8 | async-start | bytes 9437184 | tf_op jit(solution)/shard_map/reduce_scatter | solution.py:75
  15.8 1.0 copy-start.3
  15.8 1.7 copy-start.5
  102.8 1.4 copy-start
  105.6 1.0 copy-start.1
  125.0 142.7 %copy-start.8 = (f32[128]{0:T(128)S(1)}, f32[128]{0:T(128)}, u32[]{:S(2)}) copy-start(f32[128]{0:T(128)} %param.7) | copy-start | bytes 1540
  177.5 90.2 %all-to-all-start.2 = ((bf16[64,16,2,128]{3,1,2,0:T(8,128)(2,1)}), bf16[64,16,2,128]{3,1,2,0:T(8,128)(2,1)S(1)}, u32[]{:S(2)}, u32[]{:S(2)}) async-start(bf16[64,16,2,128]{3,1,2,0:T(8,128)(2,1)} %get-tuple-element.25), calls=%async_computation.3 | async-start | bytes 1048576 | tf_op jit(solution)/shard_map/all_to_all | solution.py:86
  187.1 235.7 %reduce-scatter.5.cloned.1.call-start = ((), (), s32[]{:S(2)}) async-start(), calls=%async_computation.9 | async-start | bytes 9437184 | tf_op jit(solution)/shard_map/reduce_scatter | solution.py:75
  267.8 3.8 copy-start.4
  267.8 3.8 copy-start.6
  270.6 1.0 copy-start.9
  373.5 142.2 %copy-start.7 = (bf16[512,1,1024]{2,0,1:T(8,128)(2,1)S(1)}, bf16[512,1,1024]{2,0,1:T(8,128)(2,1)}, u32[]{:S(2)}) copy-start(bf16[512,1,1024]{2,0,1:T(8,128)(2,1)} %copy-done.5) | copy-start | bytes 3145732
  426.0 89.7 %all-to-all-start.5 = ((bf16[64,16,2,128]{3,1,2,0:T(8,128)(2,1)}), bf16[64,16,2,128]{3,1,2,0:T(8,128)(2,1)S(1)}, u32[]{:S(2)}, u32[]{:S(2)}) async-start(bf16[64,16,2,128]{3,1,2,0:T(8,128)(2,1)} %get-tuple-element.23), calls=%async_computation.7 | async-start | bytes 1048576 | tf_op jit(solution)/shard_map/all_to_all | solution.py:86
Sparse Core Ops, SparseCore 0:
  125.2 49.0 reduce-scatter.2
  373.6 49.1 reduce-scatter.4
